TPU v7x, 32 devices: a whole 2x2x4 slice. The times are simulated.
32 devices in a mesh: mod: 4 (over x, core), shard: 8 (over z, y).
Axes of the slice: x: 2, y: 2, z: 4, core: 2. Of those that a mesh axis runs over, the one named last changes fastest.
Arguments:
- tokens_b: bfloat16 [512, 4096], P(('mod', 'shard')), may hold values from -6 to 6
- labels_b: int32 [512, 1], P(('mod', 'shard')), may hold values from 0 to 3; in each aligned block of 16 rows (0 to 15, 16 to 31, ...) at most 6 rows name the same one
- tokens_a: bfloat16 [512, 4096], P(('mod', 'shard')), may hold values from -6 to 6
- labels_a: int32 [512, 1], P(('mod', 'shard')), may hold values from 0 to 3; in each aligned block of 16 rows (0 to 15, 16 to 31, ...) at most 6 rows name the same one
- grad_out_a: bfloat16 [512, 4096], P(('mod', 'shard')), may hold values from -6 to 6
- gate_saved: bfloat16 [4, 192, 11008], P('mod', None, 'shard'), may hold values from -6 to 6
- up_saved: bfloat16 [4, 192, 11008], P('mod', None, 'shard'), may hold values from -6 to 6
- gate_weight: bfloat16 [4, 4096, 11008], P('mod', None, 'shard'), may hold values from -0.09375 to 0.09375
- up_weight: bfloat16 [4, 4096, 11008], P('mod', None, 'shard'), may hold values from -0.09375 to 0.09375
- down_weight: bfloat16 [4, 11008, 4096], P('mod', 'shard'), may hold values from -0.0546875 to 0.0546875
Outputs:
- output_b: bfloat16 [512, 4096], P(('mod', 'shard'))
- grad_tokens_a: bfloat16 [512, 4096], P(('mod', 'shard'))
- grad_gate: bfloat16 [4, 4096, 11008], P('mod', None, 'shard')
- grad_up: bfloat16 [4, 4096, 11008], P('mod', None, 'shard')
- grad_down: bfloat16 [4, 11008, 4096], P('mod', 'shard')
Inputs may be any that keep to these rules, and one draw needn't show every extreme that they name: `labels_b`: among the 16 tokens of one home device no label occurs more than 6 times; in every draw some home device has exactly 6 tokens of one label. `labels_a`: among the 16 tokens of one home device no label occurs more than 6 times; in every draw some home device has exactly 6 tokens of one label.
All inputs are finite; a program needn't handle non-finite values.
Results may differ from a plain program's by a relative error of at most 0.0049.
Values may be sent and summed in bfloat16 or wider, within the bound.
A program may use at most 128 MiB of HBM per device.

v0:
```python
import jax
import jax.numpy as jnp
from jax import lax
from jax.sharding import PartitionSpec as P

CAP = 6


def place_table(labels, modes):
    lab = labels[:, 0]
    onehot = (lab[:, None] == jnp.arange(modes, dtype=jnp.int32)[None, :]).astype(jnp.int32)
    rank = jnp.cumsum(onehot, axis=0) - onehot
    slot = jnp.sum(rank * onehot, axis=1)
    within = (slot[:, None] == jnp.arange(CAP, dtype=jnp.int32)[None, :]).astype(jnp.int32)
    table = onehot[:, :, None] * within[:, None, :]
    return table.reshape(lab.shape[0], modes * CAP).astype(jnp.bfloat16)


def dispatch(place, values, modes):
    sent = lax.dot_general(
        place, values, (((0,), (0,)), ((), ())), preferred_element_type=jnp.float32
    )
    return sent.astype(jnp.bfloat16).reshape(modes, CAP, values.shape[1])


def collect(place, arrived):
    flat = arrived.reshape(place.shape[1], arrived.shape[2])
    return jnp.dot(place, flat, preferred_element_type=jnp.float32).astype(jnp.bfloat16)


def contract_last(left, right):
    return lax.dot_general(
        left, right, (((1,), (1,)), ((), ())), preferred_element_type=jnp.float32
    )


def forward_pass(tokens_b, labels_b, gate_w, up_w, down_w):
    modes = lax.axis_size("mod")
    width = tokens_b.shape[1]
    place = place_table(labels_b, modes)
    sent = dispatch(place, tokens_b, modes)
    arrived = lax.all_to_all(sent, "mod", split_axis=0, concat_axis=0, tiled=True)
    local_rows = arrived.reshape(modes * CAP, width)
    piece = lax.all_gather(local_rows, "shard", axis=0, tiled=True)
    gate = jnp.dot(piece, gate_w, preferred_element_type=jnp.float32)
    up = jnp.dot(piece, up_w, preferred_element_type=jnp.float32)
    terms = jnp.dot(
        (jax.nn.silu(gate) * up).astype(jnp.bfloat16), down_w, preferred_element_type=jnp.float32
    )
    summed = lax.psum_scatter(terms, "shard", scatter_dimension=0, tiled=True)
    back = summed.astype(jnp.bfloat16).reshape(modes, CAP, width)
    returned = lax.all_to_all(back, "mod", split_axis=0, concat_axis=0, tiled=True)
    return collect(place, returned)


def backward_pass(tokens_a, labels_a, grad_out_a, gate_s, up_s, gate_w, up_w, down_w):
    modes = lax.axis_size("mod")
    width = tokens_a.shape[1]
    place = place_table(labels_a, modes)
    sent_x = dispatch(place, tokens_a, modes)
    sent_g = dispatch(place, grad_out_a, modes)
    arrived_x, arrived_g = (
        lax.all_to_all(sent_x, "mod", split_axis=0, concat_axis=0, tiled=True),
        lax.all_to_all(sent_g, "mod", split_axis=0, concat_axis=0, tiled=True),
    )
    all_x, all_g = (
        lax.all_gather(arrived_x.reshape(modes * CAP, width), "shard", axis=0, tiled=True),
        lax.all_gather(arrived_g.reshape(modes * CAP, width), "shard", axis=0, tiled=True),
    )
    gate = gate_s.astype(jnp.float32)
    up = up_s.astype(jnp.float32)
    sig = jax.nn.sigmoid(gate)
    act = gate * sig
    dh = contract_last(all_g, down_w)
    dgate = (dh * up * sig * (1.0 + gate * (1.0 - sig))).astype(jnp.bfloat16)
    dup = (dh * act).astype(jnp.bfloat16)
    hidden = (act * up).astype(jnp.bfloat16)
    outer = (((0,), (0,)), ((), ()))
    grad_down = lax.dot_general(hidden, all_g, outer, preferred_element_type=jnp.float32).astype(
        jnp.bfloat16
    )
    grad_gate = lax.dot_general(all_x, dgate, outer, preferred_element_type=jnp.float32).astype(
        jnp.bfloat16
    )
    grad_up = lax.dot_general(all_x, dup, outer, preferred_element_type=jnp.float32).astype(
        jnp.bfloat16
    )
    terms = contract_last(dgate, gate_w) + contract_last(dup, up_w)
    summed = lax.psum_scatter(terms, "shard", scatter_dimension=0, tiled=True)
    back = summed.astype(jnp.bfloat16).reshape(modes, CAP, width)
    returned = lax.all_to_all(back, "mod", split_axis=0, concat_axis=0, tiled=True)
    return (collect(place, returned), grad_gate[None], grad_up[None], grad_down[None])


def body(
    tokens_b,
    labels_b,
    tokens_a,
    labels_a,
    grad_out_a,
    gate_saved,
    up_saved,
    gate_weight,
    up_weight,
    down_weight,
):
    gate_w = gate_weight[0]
    up_w = up_weight[0]
    down_w = down_weight[0]
    output_b = forward_pass(tokens_b, labels_b, gate_w, up_w, down_w)
    grads = backward_pass(
        tokens_a, labels_a, grad_out_a, gate_saved[0], up_saved[0], gate_w, up_w, down_w
    )
    return (output_b, grads[0], grads[1], grads[2], grads[3])


def solution(mesh):
    return jax.shard_map(
        body,
        mesh=mesh,
        in_specs=(
            P(("mod", "shard"), None),
            P(("mod", "shard"), None),
            P(("mod", "shard"), None),
            P(("mod", "shard"), None),
            P(("mod", "shard"), None),
            P("mod", None, "shard"),
            P("mod", None, "shard"),
            P("mod", None, "shard"),
            P("mod", None, "shard"),
            P("mod", "shard", None),
        ),
        out_specs=(
            P(("mod", "shard"), None),
            P(("mod", "shard"), None),
            P("mod", None, "shard"),
            P("mod", None, "shard"),
            P("mod", "shard", None),
        ),
        check_vma=False,
    )
```

profile of v0, /device:TPU:0, one launch (start us, length us, event | category | flops | bytes accessed | tf_op | source)
XLA Modules:
  0.0 327.6 jit_solution(9912826482816697624)
XLA Ops:
  7.2 0.8 fusion.44
  8.2 0.8 select_reduce_fusion
  9.3 10.2 %all_to_all.25 = bf16[4,6,4096]{2,1,0:T(8,128)(2,1)S(1)} all-to-all(bf16[4,6,4096]{2,1,0:T(8,128)(2,1)S(1)} %reshape.137), channel_id=1, replica_groups=mesh['mod'=4,'shard'=8] {'mod'}, dimensions={0} | all-to-all | bytes 393216 | tf_op jit(solution)/shard_map/all_to_all | solution.py:64
  19.5 0.7 reshape.138
  21.1 8.5 %all_to_all.26 = bf16[4,6,4096]{2,1,0:T(8,128)(2,1)S(1)} all-to-all(bf16[4,6,4096]{2,1,0:T(8,128)(2,1)S(1)} %reshape.134), channel_id=1, replica_groups=mesh['mod'=4,'shard'=8] {'mod'}, dimensions={0} | all-to-all | bytes 393216 | tf_op jit(solution)/shard_map/all_to_all | solution.py:42
  29.6 0.7 reshape.135
  30.7 8.4 %all_to_all.27 = bf16[4,6,4096]{2,1,0:T(8,128)(2,1)S(1)} all-to-all(bf16[4,6,4096]{2,1,0:T(8,128)(2,1)S(1)} %reshape.140), channel_id=1, replica_groups=mesh['mod'=4,'shard'=8] {'mod'}, dimensions={0} | all-to-all | bytes 393216 | tf_op jit(solution)/shard_map/all_to_all | solution.py:63
  39.1 0.8 reshape.141
  39.9 25.0 %all-gather.6.cloned.1.call-done = bf16[192,4096]{1,0:T(8,128)(2,1)} async-done(((bf16[24,4096]{1,0:T(8,128)(2,1)}), bf16[192,4096]{1,0:T(8,128)(2,1)}) %all-gather.6.cloned.1.call-update) | async-done | bytes 1572880 | tf_op jit(solution)/shard_map/all_gather | solution.py:68
  64.9 8.9 %fusion.30 = (bf16[192,1376]{1,0:T(8,128)(2,1)S(1)}, f32[192,1376]{1,0:T(8,128)S(1)}) fusion(bf16[1,192,1376]{2,1,0:T(8,128)(2,1)S(1)} %copy-done.8, bf16[1,192,1376]{2,1,0:T(8,128)(2,1)S(1)} %copy-done.9, bf16[192,4096]{1,0:T(8,128)(2,1)} %all-gather.6.cloned.1.call-done, bf16[1,1376,4096]{2,1,0:T(8,128)(2,1)} %param.19), kind=kOutput, calls=%fused_computation.35 | convolution fusion | flops 2167431168 | bytes 15486976 | tf_op jit(solution)/shard_map/dot_general | solution.py:32
  73.9 6.2 %fusion.7 = f32[192,4096]{1,0:T(8,128)S(1)} fusion(bf16[1,4096,1376]{1,2,0:T(8,128)(2,1)} %param.18, f32[192,1376]{1,0:T(8,128)S(1)} %get-tuple-element.6, bf16[1,192,1376]{2,1,0:T(8,128)(2,1)S(1)} %copy-done.9), kind=kOutput, calls=%fused_computation.10 | convolution fusion | flops 2166110208 | bytes 16003072 | tf_op jit(solution)/shard_map/dot_general | solution.py:32
  80.1 4.5 %fusion.15 = f32[192,4096]{1,0:T(8,128)} fusion(f32[192,4096]{1,0:T(8,128)S(1)} %fusion.7, bf16[192,1376]{1,0:T(8,128)(2,1)S(1)} %get-tuple-element.5, bf16[1,4096,1376]{1,2,0:T(8,128)(2,1)S(1)} %bitcast.80), kind=kOutput, calls=%fused_computation.18 | convolution fusion | flops 2165047296 | bytes 18092032 | tf_op jit(solution)/shard_map/dot_general | solution.py:32
  84.6 0.2 reduce-scatter.3.cloned.1.call-start
  84.9 25.5 %all-gather.4.cloned.1.call-done = bf16[192,4096]{1,0:T(8,128)(2,1)} async-done(((bf16[24,4096]{1,0:T(8,128)(2,1)}), bf16[192,4096]{1,0:T(8,128)(2,1)}) %all-gather.4.cloned.1.call-update) | async-done | bytes 1572880 | tf_op jit(solution)/shard_map/all_gather | solution.py:44
  110.3 9.7 %fusion.13 = f32[192,1376]{1,0:T(8,128)} fusion(bf16[192,4096]{1,0:T(8,128)(2,1)} %all-gather.4.cloned.1.call-done, bf16[1,4096,1376]{1,2,0:T(8,128)(2,1)} %param.17), kind=kOutput, calls=%fused_computation.16 | convolution fusion | flops 2164260864 | bytes 13901824 | tf_op jit(solution)/shard_map/dot_general | solution.py:45
  120.0 15.8 %fusion.5 = f32[192,4096]{1,0:T(8,128)} fusion(bf16[1,1376,4096]{2,1,0:T(8,128)(2,1)} %param.19, bf16[192,4096]{1,0:T(8,128)(2,1)S(1)} %copy-done.7, bf16[1,4096,1376]{1,2,0:T(8,128)(2,1)} %param.18, f32[192,1376]{1,0:T(8,128)} %fusion.13), kind=kOutput, calls=%fused_computation.8 | convolution fusion | flops 4330106880 | bytes 28319744 | tf_op jit(solution)/shard_map/dot_general | solution.py:47
  135.9 1.5 copy-done.6
  137.4 7.1 %fusion = bf16[1,1376,4096]{2,1,0:T(8,128)(2,1)} fusion(bf16[192,4096]{1,0:T(8,128)(2,1)S(1)} %copy-done.6, bf16[1,192,1376]{2,1,0:T(8,128)(2,1)S(1)} %copy-done.8, bf16[1,192,1376]{2,1,0:T(8,128)(2,1)} %param.15), kind=kOutput, calls=%fused_computation.3 | convolution fusion | flops 2172010496 | bytes 13901824 | tf_op jit(solution)/shard_map/dot_general | solution.py:79
  144.6 10.6 %all-gather.8.cloned.1.call-done = bf16[192,4096]{1,0:T(8,128)(2,1)} async-done(((bf16[24,4096]{1,0:T(8,128)(2,1)}), bf16[192,4096]{1,0:T(8,128)(2,1)}) %all-gather.8.cloned.1.call-update) | async-done | bytes 1572880 | tf_op jit(solution)/shard_map/all_gather | solution.py:67
  155.1 9.5 %fusion.2 = bf16[1,4096,1376]{1,2,0:T(8,128)(2,1)} fusion(bf16[192,4096]{1,0:T(8,128)(2,1)} %all-gather.8.cloned.1.call-done, f32[192,1376]{1,0:T(8,128)} %copy-done.10, bf16[1,192,1376]{2,1,0:T(8,128)(2,1)} %param.15), kind=kOutput, calls=%fused_computation.5 | convolution fusion | flops 2171746304 | bytes 14430208 | tf_op jit(solution)/shard_map/dot_general | solution.py:85
  164.6 67.3 %reduce-scatter.5.cloned.1.call-done = f32[24,4096]{1,0:T(8,128)} async-done(((f32[192,4096]{1,0:T(8,128)}), f32[24,4096]{1,0:T(8,128)}) %reduce-scatter.5.cloned.1.call-update) | async-done | bytes 393232 | tf_op jit(solution)/shard_map/reduce_scatter | solution.py:89
  231.9 1.0 convert_element_type.115
  232.9 0.8 reshape.139
  233.7 3.4 %all-to-all-start.3 = ((bf16[4,6,4096]{2,1,0:T(8,128)(2,1)}), bf16[4,6,4096]{2,1,0:T(8,128)(2,1)S(1)}, u32[]{:S(2)}, u32[]{:S(2)}) async-start(bf16[4,6,4096]{2,1,0:T(8,128)(2,1)} %reshape.139), calls=%async_computation.5 | async-start | bytes 524288 | tf_op jit(solution)/shard_map/all_to_all | solution.py:91
  237.1 6.0 %fusion.1 = bf16[1,4096,1376]{1,2,0:T(8,128)(2,1)} fusion(bf16[192,4096]{1,0:T(8,128)(2,1)S(1)} %copy-done.2, bf16[192,1376]{1,0:T(8,128)(2,1)S(1)} %get-tuple-element.5), kind=kOutput, calls=%fused_computation.4 | convolution fusion | flops 2169896960 | bytes 13373440 | tf_op jit(solution)/shard_map/dot_general | solution.py:82
  243.2 65.8 %reduce-scatter.3.cloned.1.call-done = f32[24,4096]{1,0:T(8,128)} async-done(((f32[192,4096]{1,0:T(8,128)}), f32[24,4096]{1,0:T(8,128)}) %reduce-scatter.3.cloned.1.call-update) | async-done | bytes 393232 | tf_op jit(solution)/shard_map/reduce_scatter | solution.py:50
  309.0 1.0 convert_element_type.102
  310.0 0.8 reshape.136
  310.8 3.4 %all-to-all-start.1 = ((bf16[4,6,4096]{2,1,0:T(8,128)(2,1)}), bf16[4,6,4096]{2,1,0:T(8,128)(2,1)S(1)}, u32[]{:S(2)}, u32[]{:S(2)}) async-start(bf16[4,6,4096]{2,1,0:T(8,128)(2,1)} %reshape.136), calls=%async_computation.2 | async-start | bytes 524288 | tf_op jit(solution)/shard_map/all_to_all | solution.py:52
  314.2 0.9 fusion.19
  315.1 5.1 %all-to-all-done.1 = bf16[4,6,4096]{2,1,0:T(8,128)(2,1)S(1)} async-done(((bf16[4,6,4096]{2,1,0:T(8,128)(2,1)}), bf16[4,6,4096]{2,1,0:T(8,128)(2,1)S(1)}, u32[]{:S(2)}, u32[]{:S(2)}) %all-to-all-start.1) | async-done | bytes 196640 | tf_op jit(solution)/shard_map/all_to_all | solution.py:52
  320.2 0.9 fusion.18
  (56 shorter events, 1.6 us)
Async XLA Ops:
  7.2 1.9 copy-start
  7.2 13.1 %copy-start.5 = (s32[16,1]{0,1:T(1,128)S(1)}, s32[16,1]{0,1:T(1,128)}, u32[]{:S(2)}) copy-start(s32[16,1]{0,1:T(1,128)} %param.11) | copy-start | bytes 196
  7.2 13.6 %copy-start.3 = (bf16[16,4096]{1,0:T(8,128)(2,1)S(1)}, bf16[16,4096]{1,0:T(8,128)(2,1)}, u32[]{:S(2)}) copy-start(bf16[16,4096]{1,0:T(8,128)(2,1)} %param.10) | copy-start | bytes 393220
  7.2 57.7 %all-gather.6.cloned.1.call-start = ((), (), s32[]{:S(2)}) async-start(), calls=%async_computation.9 | async-start | bytes 1769472 | tf_op jit(solution)/shard_map/all_gather | solution.py:68
  9.3 21.1 %copy-start.4 = (bf16[16,4096]{1,0:T(8,128)(2,1)S(1)}, bf16[16,4096]{1,0:T(8,128)(2,1)}, u32[]{:S(2)}) copy-start(bf16[16,4096]{1,0:T(8,128)(2,1)} %param.12) | copy-start | bytes 393220
  20.3 90.0 %all-gather.4.cloned.1.call-start = ((), (), s32[]{:S(2)}) async-start(), calls=%async_computation.7 | async-start | bytes 1769472 | tf_op jit(solution)/shard_map/all_gather | solution.py:44
  21.0 43.9 %copy-start.8 = (bf16[1,192,1376]{2,1,0:T(8,128)(2,1)S(1)}, bf16[1,192,1376]{2,1,0:T(8,128)(2,1)}, u32[]{:S(2)}) copy-start(bf16[1,192,1376]{2,1,0:T(8,128)(2,1)} %param.16) | copy-start | bytes 1585156
  21.0 43.9 %copy-start.9 = (bf16[1,192,1376]{2,1,0:T(8,128)(2,1)S(1)}, bf16[1,192,1376]{2,1,0:T(8,128)(2,1)}, u32[]{:S(2)}) copy-start(bf16[1,192,1376]{2,1,0:T(8,128)(2,1)} %param.15) | copy-start | bytes 1585156
  30.4 124.8 %all-gather.8.cloned.1.call-start = ((), (), s32[]{:S(2)}) async-start(), calls=%async_computation.11 | async-start | bytes 1769472 | tf_op jit(solution)/shard_map/all_gather | solution.py:67
  39.9 192.0 %reduce-scatter.5.cloned.1.call-start = ((), (), s32[]{:S(2)}) async-start(), calls=%async_computation.10 | async-start | bytes 3538944 | tf_op jit(solution)/shard_map/reduce_scatter | solution.py:89
  64.9 15.2 %slice-start = ((s8[11272192]{0:T(1024)(128)(4,1)}), s8[4194304]{0:T(1024)(128)(4,1)S(1)}, s32[]{:S(2)}) async-start(s8[11272192]{0:T(1024)(128)(4,1)} %bitcast.79), calls=%async_computation.12 | async-start | bytes 8388608
  64.9 15.2 %slice-start.1 = ((s8[11272192]{0:T(1024)(128)(4,1)}), s8[2883584]{0:T(1024)(128)(4,1)S(1)}, s32[]{:S(2)}) async-start(s8[11272192]{0:T(1024)(128)(4,1)} %bitcast.79), calls=%async_computation.13 | async-start | bytes 5767168
  73.8 6.3 %copy-start.10 = (f32[192,1376]{1,0:T(8,128)}, f32[192,1376]{1,0:T(8,128)S(1)}, u32[]{:S(2)}) copy-start(f32[192,1376]{1,0:T(8,128)S(1)} %get-tuple-element.6) | copy-start | bytes 3170308
  73.9 6.3 %slice-start.2 = ((s8[11272192]{0:T(1024)(128)(4,1)}), s8[4194304]{0:T(1024)(128)(4,1)S(1)}, s32[]{:S(2)}) async-start(s8[11272192]{0:T(1024)(128)(4,1)} %bitcast.79), calls=%async_computation.14 | async-start | bytes 8388608
  84.6 224.4 %reduce-scatter.3.cloned.1.call-start = ((), (), s32[]{:S(2)}) async-start(), calls=%async_computation.8 | async-start | bytes 3538944 | tf_op jit(solution)/shard_map/reduce_scatter | solution.py:50
  110.3 9.7 %copy-start.7 = (bf16[192,4096]{1,0:T(8,128)(2,1)S(1)}, bf16[192,4096]{1,0:T(8,128)(2,1)}, u32[]{:S(2)}) copy-start(bf16[192,4096]{1,0:T(8,128)(2,1)} %all-gather.4.cloned.1.call-done) | copy-start | bytes 4718596
  135.9 1.6 copy-start.6
  155.1 82.0 %copy-start.2 = (bf16[192,4096]{1,0:T(8,128)(2,1)S(1)}, bf16[192,4096]{1,0:T(8,128)(2,1)}, u32[]{:S(2)}) copy-start(bf16[192,4096]{1,0:T(8,128)(2,1)} %all-gather.8.cloned.1.call-done) | copy-start | bytes 4718596
  233.7 77.1 %all-to-all-start.3 = ((bf16[4,6,4096]{2,1,0:T(8,128)(2,1)}), bf16[4,6,4096]{2,1,0:T(8,128)(2,1)S(1)}, u32[]{:S(2)}, u32[]{:S(2)}) async-start(bf16[4,6,4096]{2,1,0:T(8,128)(2,1)} %reshape.139), calls=%async_computation.5 | async-start | bytes 524288 | tf_op jit(solution)/shard_map/all_to_all | solution.py:91
  237.1 83.9 %copy-start.1 = (bf16[16,4096]{1,0:T(8,128)(2,1)S(1)}, bf16[16,4096]{1,0:T(8,128)(2,1)}, u32[]{:S(2)}) copy-start(bf16[16,4096]{1,0:T(8,128)(2,1)} %param.14) | copy-start | bytes 393220
  310.8 9.4 %all-to-all-start.1 = ((bf16[4,6,4096]{2,1,0:T(8,128)(2,1)}), bf16[4,6,4096]{2,1,0:T(8,128)(2,1)S(1)}, u32[]{:S(2)}, u32[]{:S(2)}) async-start(bf16[4,6,4096]{2,1,0:T(8,128)(2,1)} %reshape.136), calls=%async_computation.2 | async-start | bytes 524288 | tf_op jit(solution)/shard_map/all_to_all | solution.py:52
Sparse Core Ops, SparseCore 0:
  20.4 44.4 all-gather.5
  67.7 42.5 all-gather.3
  112.5 42.5 all-gather.7
  159.1 72.7 reduce-scatter.4
  235.3 73.6 reduce-scatter.2
where the time goes:
time: 328 us
  waiting for transfers between devices  199 us (61%)
  matrix products  70.1 us (21%)
  blocking collectives  27.1 us (8%)
  between operations  14 us (4%)
  starting transfers between devices  7.2 us (2%)
  local copies, waits for them, and re-layouts  5.84 us (2%)
  other arithmetic  4.02 us (1%)
    reduce_scatter x1, waiting for transfers between devices, backward_pass(): summed = lax.psum_scatter(terms, 'shard', scatter_dimension=0, tiled=True)  67.3 us
    reduce_scatter x1, waiting for transfers between devices, forward_pass(): summed = lax.psum_scatter(terms, 'shard', scatter_dimension=0, tiled=True)  65.8 us
    all_gather x1, waiting for transfers between devices, forward_pass(): piece = lax.all_gather(local_rows, 'shard', axis=0, tiled=True)  25.5 us
    all_gather x1, waiting for transfers between devices, backward_pass(): lax.all_gather(arrived_g.reshape(modes * CAP, width), 'shard', axis=0, ti...  25 us
    dot_general x3, matrix products, contract_last(): lax.dot_general(left, right, (((1,), (1,)), ((), ())), preferred_element_...  19.6 us
    dot_general x1, matrix products, forward_pass(): jnp.dot((jax.nn.silu(gate) * up).astype(jnp.bfloat16), down_w, preferred_...  15.8 us
    all_gather x1, waiting for transfers between devices, backward_pass(): lax.all_gather(arrived_x.reshape(modes * CAP, width), 'shard', axis=0, ti...  10.6 us
    all_to_all x1, blocking collectives, backward_pass(): lax.all_to_all(sent_g, 'mod', split_axis=0, concat_axis=0, tiled=True)  10.2 us
  transfers between devices with their start and end apart: 7, of which 6 were waited for; matrix products, arithmetic and copies ran while one was open for 23% of the time, Pallas kernels for 0%

commit v1 on v0

v1 whole, which is shorter than its diff:
```python
import jax
import jax.numpy as jnp
from jax import lax
from jax.sharding import PartitionSpec as P

CAP = 6


def place_table(labels, modes):
    lab = labels[:, 0]
    onehot = (lab[:, None] == jnp.arange(modes, dtype=jnp.int32)[None, :]).astype(jnp.int32)
    rank = jnp.cumsum(onehot, axis=0) - onehot
    slot = jnp.sum(rank * onehot, axis=1)
    within = (slot[:, None] == jnp.arange(CAP, dtype=jnp.int32)[None, :]).astype(jnp.int32)
    table = onehot[:, :, None] * within[:, None, :]
    return table.reshape(lab.shape[0], modes * CAP).astype(jnp.bfloat16)


def dispatch(place, values, modes):
    sent = lax.dot_general(
        place, values, (((0,), (0,)), ((), ())), preferred_element_type=jnp.float32
    )
    return sent.astype(jnp.bfloat16).reshape(modes, CAP, values.shape[1])


def collect(place, arrived):
    flat = arrived.reshape(place.shape[1], arrived.shape[2])
    return jnp.dot(place, flat, preferred_element_type=jnp.float32).astype(jnp.bfloat16)


def contract_last(left, right):
    return lax.dot_general(
        left, right, (((1,), (1,)), ((), ())), preferred_element_type=jnp.float32
    )


def silu_mul(gate, up):
    return (jax.nn.silu(gate) * up).astype(jnp.bfloat16)


def body(
    tokens_b,
    labels_b,
    tokens_a,
    labels_a,
    grad_out_a,
    gate_saved,
    up_saved,
    gate_weight,
    up_weight,
    down_weight,
):
    gate_w, up_w, down_w = gate_weight[0], up_weight[0], down_weight[0]
    gate_s, up_s = gate_saved[0], up_saved[0]
    modes = lax.axis_size("mod")
    width = tokens_b.shape[1]
    rows = modes * CAP
    tie = lax.optimization_barrier

    place_a = place_table(labels_a, modes)
    place_b = place_table(labels_b, modes)

    def to_group(value):
        return lax.all_to_all(value, "mod", split_axis=0, concat_axis=0, tiled=True)

    def gather(value):
        return lax.all_gather(value, "shard", axis=0, tiled=True)

    arrived_g = to_group(dispatch(place_a, grad_out_a, modes))
    all_g = gather(arrived_g.reshape(rows, width))
    sent_rest = jnp.concatenate(
        [dispatch(place_b, tokens_b, modes), dispatch(place_a, tokens_a, modes)], axis=1
    )
    sent_rest, arrived_g = tie((sent_rest, arrived_g))
    arrived_rest = to_group(sent_rest)
    all_b = gather(arrived_rest[:, :CAP].reshape(rows, width))
    local_x = arrived_rest[:, CAP:].reshape(rows, width)

    gate = gate_s.astype(jnp.float32)
    up = up_s.astype(jnp.float32)
    sig = jax.nn.sigmoid(gate)
    act = gate * sig
    dh = contract_last(all_g, down_w)
    dgate = (dh * up * sig * (1.0 + gate * (1.0 - sig))).astype(jnp.bfloat16)
    dup = (dh * act).astype(jnp.bfloat16)
    hidden = (act * up).astype(jnp.bfloat16)
    terms_a = (contract_last(dgate, gate_w) + contract_last(dup, up_w)).astype(jnp.bfloat16)

    all_b, local_x, terms_a = tie((all_b, local_x, terms_a))
    summed_a = lax.psum_scatter(terms_a, "shard", scatter_dimension=0, tiled=True)
    all_x = gather(local_x)
    fwd_gate = jnp.dot(all_b, gate_w, preferred_element_type=jnp.float32)
    fwd_up = jnp.dot(all_b, up_w, preferred_element_type=jnp.float32)
    terms_b = jnp.dot(
        silu_mul(fwd_gate, fwd_up), down_w, preferred_element_type=jnp.float32
    ).astype(jnp.bfloat16)

    all_x, hidden, terms_b = tie((all_x, hidden, terms_b))
    summed_b = lax.psum_scatter(terms_b, "shard", scatter_dimension=0, tiled=True)
    outer = (((0,), (0,)), ((), ()))

    def weight_grad(left, right):
        return lax.dot_general(left, right, outer, preferred_element_type=jnp.float32).astype(
            jnp.bfloat16
        )

    grad_down = weight_grad(hidden, all_g)
    grad_gate = weight_grad(all_x, dgate)
    grad_up = weight_grad(all_x, dup)
    back_a = to_group(summed_a.reshape(modes, CAP, width))
    back_b = to_group(summed_b.reshape(modes, CAP, width))
    return (
        collect(place_b, back_b),
        collect(place_a, back_a),
        grad_gate[None],
        grad_up[None],
        grad_down[None],
    )


def solution(mesh):
    return jax.shard_map(
        body,
        mesh=mesh,
        in_specs=(
            P(("mod", "shard"), None),
            P(("mod", "shard"), None),
            P(("mod", "shard"), None),
            P(("mod", "shard"), None),
            P(("mod", "shard"), None),
            P("mod", None, "shard"),
            P("mod", None, "shard"),
            P("mod", None, "shard"),
            P("mod", None, "shard"),
            P("mod", "shard", None),
        ),
        out_specs=(
            P(("mod", "shard"), None),
            P(("mod", "shard"), None),
            P("mod", None, "shard"),
            P("mod", None, "shard"),
            P("mod", "shard", None),
        ),
        check_vma=False,
    )
```

time: 328 us -> 310 us (0.945)
  waiting for transfers between devices: 199 us -> 190 us
  blocking collectives: 27.1 us -> 21.4 us
  matrix products: 70.1 us -> 66.8 us
    reduce_scatter x2, waiting for transfers between devices: 133 us -> 108 us  [the longest x1 54.3 us: body(): lax.psum_scatter(terms_a, 'shard', scatter_dimension=0, tiled=True)]
    all_gather x3, waiting for transfers between devices: 61.1 us -> 76.1 us  [gather(): return lax.all_gather(value, 'shard', axis=0, tiled=True)]
    all_to_all x3 -> x2, blocking collectives: 27.1 us -> 21.4 us  [to_group(): return lax.all_to_all(value, 'mod', split_axis=0, concat_axis=0, tiled=True)]
where the time goes in v1:
time: 310 us
  waiting for transfers between devices  190 us (61%)
  matrix products  66.8 us (22%)
  blocking collectives  21.4 us (7%)
  between operations  14 us (5%)
  local copies, waits for them, and re-layouts  8.16 us (3%)
  starting transfers between devices  7.41 us (2%)
    all_gather x3, waiting for transfers between devices, gather(): return lax.all_gather(value, 'shard', axis=0, tiled=True)  76.1 us
    reduce_scatter x1, waiting for transfers between devices, body(): lax.psum_scatter(terms_a, 'shard', scatter_dimension=0, tiled=True)  54.3 us
    reduce_scatter x1, waiting for transfers between devices, body(): lax.psum_scatter(terms_b, 'shard', scatter_dimension=0, tiled=True)  53.4 us
    all_to_all x2, blocking collectives, to_group(): return lax.all_to_all(value, 'mod', split_axis=0, concat_axis=0, tiled=True)  21.4 us
    dot_general x3, matrix products, weight_grad(): lax.dot_general(left, right, outer, preferred_element_type=jnp.float32)  21 us
    dot_general x3, matrix products, contract_last(): lax.dot_general(left, right, (((1,), (1,)), ((), ())), preferred_element_...  19 us
    dot_general x1, matrix products, body(): jnp.dot(silu_mul(fwd_gate, fwd_up), down_w, preferred_element_type=jnp.fl...  15.3 us
    dot_general x1, matrix products, body(): fwd_gate = jnp.dot(all_b, gate_w, preferred_element_type=jnp.float32)  9.12 us
  transfers between devices with their start and end apart: 7, of which 6 were waited for; matrix products, arithmetic and copies ran while one was open for 23% of the time, Pallas kernels for 0%

profile of v1, /device:TPU:0, one launch (start us, length us, event | category | flops | bytes accessed | tf_op | source)
XLA Modules:
  0.0 309.5 jit_solution(6139204313617867293)
XLA Ops:
  7.3 0.8 fusion.48
  8.2 0.8 select_reduce_fusion
  9.4 10.0 %all_to_all.20 = bf16[4,6,4096]{2,1,0:T(8,128)(2,1)S(1)} all-to-all(bf16[4,6,4096]{2,1,0:T(8,128)(2,1)S(1)} %reshape.136), channel_id=1, replica_groups=mesh['mod'=4,'shard'=8] {'mod'}, dimensions={0} | all-to-all | bytes 393216 | tf_op jit(solution)/shard_map/all_to_all | solution.py:64
  19.4 0.7 reshape.139
  20.7 0.2 convolution_convert_fusion.5
  21.4 11.3 %all_to_all.21 = bf16[4,12,4096]{2,1,0:T(8,128)(2,1)S(1)} all-to-all(bf16[4,12,4096]{2,1,0:T(8,128)(2,1)S(1)} %pad_maximum_fusion), channel_id=1, replica_groups=mesh['mod'=4,'shard'=8] {'mod'}, dimensions={0} | all-to-all | bytes 786432 | tf_op jit(solution)/shard_map/all_to_all | solution.py:64
  32.9 0.7 reshape.138
  33.6 0.7 reshape.137
  34.4 30.4 %all-gather.6.cloned.1.call-done = bf16[192,4096]{1,0:T(8,128)(2,1)} async-done(((bf16[24,4096]{1,0:T(8,128)(2,1)}), bf16[192,4096]{1,0:T(8,128)(2,1)}) %all-gather.6.cloned.1.call-update) | async-done | bytes 1572880 | tf_op jit(solution)/shard_map/all_gather | solution.py:67
  64.8 8.9 %fusion.37 = (bf16[192,1376]{1,0:T(8,128)(2,1)S(1)}, bf16[192,1376]{1,0:T(8,128)(2,1)S(1)}, f32[192,1376]{1,0:T(8,128)S(1)}) fusion(bf16[1,192,1376]{2,1,0:T(8,128)(2,1)S(1)} %copy-done.7, bf16[1,192,1376]{2,1,0:T(8,128)(2,1)S(1)} %copy-done.8, bf16[192,4096]{1,0:T(8,128)(2,1)} %all-gather.6.cloned.1.call-done, bf16[1,1376,4096]{2,1,0:T(8,128)(2,1)} %param.19), kind=kOutput, calls=%fused_computation.38 | convolution fusion | flops 2168223744 | bytes 16015360 | tf_op jit(solution)/shard_map/dot_general | solution.py:32
  73.7 6.2 %fusion.5 = f32[192,4096]{1,0:T(8,128)S(1)} fusion(bf16[1,4096,1376]{1,2,0:T(8,128)(2,1)} %param.18, f32[192,1376]{1,0:T(8,128)S(1)} %get-tuple-element.23, bf16[1,192,1376]{2,1,0:T(8,128)(2,1)S(1)} %copy-done.8), kind=kOutput, calls=%fused_computation.8 | convolution fusion | flops 2166110208 | bytes 16003072 | tf_op jit(solution)/shard_map/dot_general | solution.py:32
  80.0 3.9 %fusion.21 = bf16[192,4096]{1,0:T(8,128)(2,1)} fusion(f32[192,4096]{1,0:T(8,128)S(1)} %fusion.5, bf16[192,1376]{1,0:T(8,128)(2,1)S(1)} %get-tuple-element.20, bf16[1,4096,1376]{1,2,0:T(8,128)(2,1)S(1)} %bitcast.81), kind=kOutput, calls=%fused_computation.20 | convolution fusion | flops 2165833728 | bytes 16519168 | tf_op jit(solution)/shard_map/dot_general | solution.py:32
  83.9 26.3 %all-gather.4.cloned.1.call-done = bf16[192,4096]{1,0:T(8,128)(2,1)} async-done(((bf16[24,4096]{1,0:T(8,128)(2,1)}), bf16[192,4096]{1,0:T(8,128)(2,1)}) %all-gather.4.cloned.1.call-update) | async-done | bytes 1572880 | tf_op jit(solution)/shard_map/all_gather | solution.py:67
  110.2 0.5 reduce-scatter.5.cloned.1.call-update
  110.8 0.2 reduce-scatter.3.cloned.1.call-start
  111.0 0.6 copy-done.6
  111.6 9.1 %fusion.7 = f32[192,1376]{1,0:T(8,128)} fusion(bf16[192,4096]{1,0:T(8,128)(2,1)S(1)} %copy-done.6, bf16[1,4096,1376]{1,2,0:T(8,128)(2,1)} %param.17), kind=kOutput, calls=%fused_computation.10 | convolution fusion | flops 2164260864 | bytes 13901824 | tf_op jit(solution)/shard_map/dot_general | solution.py:92
  120.7 15.3 %fusion.15 = bf16[192,4096]{1,0:T(8,128)(2,1)} fusion(bf16[1,1376,4096]{2,1,0:T(8,128)(2,1)} %param.19, bf16[192,4096]{1,0:T(8,128)(2,1)S(1)} %copy-done.6, bf16[1,4096,1376]{1,2,0:T(8,128)(2,1)} %param.18, f32[192,1376]{1,0:T(8,128)} %fusion.7), kind=kOutput, calls=%fused_computation.18 | convolution fusion | flops 4330893312 | bytes 26746880 | tf_op jit(solution)/shard_map/dot_general | solution.py:94
  136.0 19.5 %all-gather.8.cloned.1.call-done = bf16[192,4096]{1,0:T(8,128)(2,1)} async-done(((bf16[24,4096]{1,0:T(8,128)(2,1)}), bf16[192,4096]{1,0:T(8,128)(2,1)}) %all-gather.8.cloned.1.call-update) | async-done | bytes 1572880 | tf_op jit(solution)/shard_map/all_gather | solution.py:67
  155.5 1.4 copy-done.2
  156.9 6.0 %fusion.1 = bf16[1,4096,1376]{1,2,0:T(8,128)(2,1)} fusion(bf16[192,4096]{1,0:T(8,128)(2,1)S(1)} %copy-done.2, bf16[192,1376]{1,0:T(8,128)(2,1)S(1)} %get-tuple-element.20), kind=kOutput, calls=%fused_computation.4 | convolution fusion | flops 2169896960 | bytes 13373440 | tf_op jit(solution)/shard_map/dot_general | solution.py:103
  162.9 6.1 %fusion.2 = bf16[1,4096,1376]{1,2,0:T(8,128)(2,1)} fusion(bf16[192,4096]{1,0:T(8,128)(2,1)S(1)} %copy-done.2, f32[192,1376]{1,0:T(8,128)S(1)} %copy-done.10, bf16[1,192,1376]{2,1,0:T(8,128)(2,1)S(1)} %copy-done.8), kind=kOutput, calls=%fused_computation.5 | convolution fusion | flops 2171746304 | bytes 14430208 | tf_op jit(solution)/shard_map/dot_general | solution.py:103
  169.0 54.3 %reduce-scatter.5.cloned.1.call-done = bf16[24,4096]{1,0:T(8,128)(2,1)} async-done(((bf16[192,4096]{1,0:T(8,128)(2,1)}), bf16[24,4096]{1,0:T(8,128)(2,1)}) %reduce-scatter.5.cloned.1.call-update) | async-done | bytes 196624 | tf_op jit(solution)/shard_map/reduce_scatter | solution.py:90
  223.3 1.7 reshape.141
  225.0 3.6 %all-to-all-start.3 = ((bf16[4,6,4096]{2,1,0:T(8,128)(2,1)}), bf16[4,6,4096]{2,1,0:T(8,128)(2,1)S(1)}, u32[]{:S(2)}, u32[]{:S(2)}) async-start(bf16[4,6,4096]{2,1,0:T(8,128)(2,1)} %reshape.141), calls=%async_computation.5 | async-start | bytes 524288 | tf_op jit(solution)/shard_map/all_to_all | solution.py:64
  228.7 8.9 %fusion = bf16[1,1376,4096]{2,1,0:T(8,128)(2,1)} fusion(bf16[192,1376]{1,0:T(8,128)(2,1)S(1)} %get-tuple-element.18, bf16[192,4096]{1,0:T(8,128)(2,1)} %all-gather.6.cloned.1.call-done), kind=kOutput, calls=%fused_computation.3 | convolution fusion | flops 2169896960 | bytes 13373440 | tf_op jit(solution)/shard_map/dot_general | solution.py:103
  237.6 53.4 %reduce-scatter.3.cloned.1.call-done = bf16[24,4096]{1,0:T(8,128)(2,1)} async-done(((bf16[192,4096]{1,0:T(8,128)(2,1)}), bf16[24,4096]{1,0:T(8,128)(2,1)}) %reduce-scatter.3.cloned.1.call-update) | async-done | bytes 196624 | tf_op jit(solution)/shard_map/reduce_scatter | solution.py:99
  291.0 1.7 reshape.140
  292.7 3.4 %all-to-all-start.2 = ((bf16[4,6,4096]{2,1,0:T(8,128)(2,1)}), bf16[4,6,4096]{2,1,0:T(8,128)(2,1)S(1)}, u32[]{:S(2)}, u32[]{:S(2)}) async-start(bf16[4,6,4096]{2,1,0:T(8,128)(2,1)} %reshape.140), calls=%async_computation.3 | async-start | bytes 524288 | tf_op jit(solution)/shard_map/all_to_all | solution.py:64
  296.1 0.9 fusion.25
  297.0 5.1 %all-to-all-done.2 = bf16[4,6,4096]{2,1,0:T(8,128)(2,1)S(1)} async-done(((bf16[4,6,4096]{2,1,0:T(8,128)(2,1)}), bf16[4,6,4096]{2,1,0:T(8,128)(2,1)S(1)}, u32[]{:S(2)}, u32[]{:S(2)}) %all-to-all-start.2) | async-done | bytes 196640 | tf_op jit(solution)/shard_map/all_to_all | solution.py:64
  302.1 0.9 fusion.24
  (55 shorter events, 1.7 us)
Async XLA Ops:
  7.2 1.9 copy-start
  7.2 13.1 %copy-start.5 = (s32[16,1]{0,1:T(1,128)S(1)}, s32[16,1]{0,1:T(1,128)}, u32[]{:S(2)}) copy-start(s32[16,1]{0,1:T(1,128)} %param.11) | copy-start | bytes 196
  7.2 13.5 %copy-start.3 = (bf16[16,4096]{1,0:T(8,128)(2,1)S(1)}, bf16[16,4096]{1,0:T(8,128)(2,1)}, u32[]{:S(2)}) copy-start(bf16[16,4096]{1,0:T(8,128)(2,1)} %param.10) | copy-start | bytes 393220
  7.2 13.8 %copy-start.4 = (bf16[16,4096]{1,0:T(8,128)(2,1)S(1)}, bf16[16,4096]{1,0:T(8,128)(2,1)}, u32[]{:S(2)}) copy-start(bf16[16,4096]{1,0:T(8,128)(2,1)} %param.12) | copy-start | bytes 393220
  7.2 57.6 %all-gather.6.cloned.1.call-start = ((), (), s32[]{:S(2)}) async-start(), calls=%async_computation.7 | async-start | bytes 1769472 | tf_op jit(solution)/shard_map/all_gather | solution.py:67
  20.2 90.0 %all-gather.4.cloned.1.call-start = ((), (), s32[]{:S(2)}) async-start(), calls=%async_computation.6 | async-start | bytes 1769472 | tf_op jit(solution)/shard_map/all_gather | solution.py:67
  21.4 43.4 %copy-start.7 = (bf16[1,192,1376]{2,1,0:T(8,128)(2,1)S(1)}, bf16[1,192,1376]{2,1,0:T(8,128)(2,1)}, u32[]{:S(2)}) copy-start(bf16[1,192,1376]{2,1,0:T(8,128)(2,1)} %param.16) | copy-start | bytes 1585156
  21.4 43.4 %copy-start.8 = (bf16[1,192,1376]{2,1,0:T(8,128)(2,1)S(1)}, bf16[1,192,1376]{2,1,0:T(8,128)(2,1)}, u32[]{:S(2)}) copy-start(bf16[1,192,1376]{2,1,0:T(8,128)(2,1)} %param.15) | copy-start | bytes 1585156
  34.4 121.1 %all-gather.8.cloned.1.call-start = ((), (), s32[]{:S(2)}) async-start(), calls=%async_computation.8 | async-start | bytes 1769472 | tf_op jit(solution)/shard_map/all_gather | solution.py:67
  64.8 15.1 %slice-start = ((s8[11272192]{0:T(1024)(128)(4,1)}), s8[4194304]{0:T(1024)(128)(4,1)S(1)}, s32[]{:S(2)}) async-start(s8[11272192]{0:T(1024)(128)(4,1)} %bitcast.80), calls=%async_computation.11 | async-start | bytes 8388608
  64.8 15.2 %slice-start.1 = ((s8[11272192]{0:T(1024)(128)(4,1)}), s8[2883584]{0:T(1024)(128)(4,1)S(1)}, s32[]{:S(2)}) async-start(s8[11272192]{0:T(1024)(128)(4,1)} %bitcast.80), calls=%async_computation.12 | async-start | bytes 5767168
  73.7 6.2 %copy-start.9 = (f32[192,1376]{1,0:T(8,128)}, f32[192,1376]{1,0:T(8,128)S(1)}, u32[]{:S(2)}) copy-start(f32[192,1376]{1,0:T(8,128)S(1)} %get-tuple-element.23) | copy-start | bytes 3170308
  73.7 6.3 %slice-start.2 = ((s8[11272192]{0:T(1024)(128)(4,1)}), s8[4194304]{0:T(1024)(128)(4,1)S(1)}, s32[]{:S(2)}) async-start(s8[11272192]{0:T(1024)(128)(4,1)} %bitcast.80), calls=%async_computation.13 | async-start | bytes 8388608
  110.2 1.4 copy-start.6
  110.2 113.1 %reduce-scatter.5.cloned.1.call-start = ((), (), s32[]{:S(2)}) async-start(), calls=%async_computation.10 | async-start | bytes 1769472 | tf_op jit(solution)/shard_map/reduce_scatter | solution.py:90
  110.8 180.2 %reduce-scatter.3.cloned.1.call-start = ((), (), s32[]{:S(2)}) async-start(), calls=%async_computation.9 | async-start | bytes 1769472 | tf_op jit(solution)/shard_map/reduce_scatter | solution.py:99
  155.5 1.4 copy-start.2
  156.9 6.0 %copy-start.10 = (f32[192,1376]{1,0:T(8,128)S(1)}, f32[192,1376]{1,0:T(8,128)}, u32[]{:S(2)}) copy-start(f32[192,1376]{1,0:T(8,128)} %copy-done.9) | copy-start | bytes 3170308
  225.0 67.7 %all-to-all-start.3 = ((bf16[4,6,4096]{2,1,0:T(8,128)(2,1)}), bf16[4,6,4096]{2,1,0:T(8,128)(2,1)S(1)}, u32[]{:S(2)}, u32[]{:S(2)}) async-start(bf16[4,6,4096]{2,1,0:T(8,128)(2,1)} %reshape.141), calls=%async_computation.5 | async-start | bytes 524288 | tf_op jit(solution)/shard_map/all_to_all | solution.py:64
  228.7 74.3 %copy-start.1 = (bf16[16,4096]{1,0:T(8,128)(2,1)S(1)}, bf16[16,4096]{1,0:T(8,128)(2,1)}, u32[]{:S(2)}) copy-start(bf16[16,4096]{1,0:T(8,128)(2,1)} %param.14) | copy-start | bytes 393220
  292.7 9.4 %all-to-all-start.2 = ((bf16[4,6,4096]{2,1,0:T(8,128)(2,1)}), bf16[4,6,4096]{2,1,0:T(8,128)(2,1)S(1)}, u32[]{:S(2)}, u32[]{:S(2)}) async-start(bf16[4,6,4096]{2,1,0:T(8,128)(2,1)} %reshape.140), calls=%async_computation.3 | async-start | bytes 524288 | tf_op jit(solution)/shard_map/all_to_all | solution.py:64
Sparse Core Ops, SparseCore 0:
  20.3 44.4 all-gather.5
  67.6 42.5 all-gather.3
  112.9 42.5 all-gather.7
  159.4 63.9 reduce-scatter.4
  226.6 64.3 reduce-scatter.2
